TPU v7x, 32 devices: a whole 2x2x4 slice. The times are simulated.
32 devices in a mesh: dp: 4 (over z), vocab: 8 (over y, x, core).
Axes of the slice: x: 2, y: 2, z: 4, core: 2. Of those that a mesh axis runs over, the one named last changes fastest.
Arguments:
- hidden: bfloat16 [2560, 4096], P(('dp', 'vocab')), may hold values from -192 to 192, as said below
- out_weight: bfloat16 [4096, 20480], P('dp', 'vocab'), may hold values from -0.09375 to 0.09375
- labels: int32 [2560], P('dp'), may hold values from 0 to 20479
- text_mask: int32 [2560], P('dp'), may hold values from 0 to 1, as said below
Outputs:
- token_loss: float32 [2560], P('dp')
- mean_loss: float32 [], replicated
Inputs may be any that keep to these rules, and one draw needn't show every extreme that they name: The hidden states are of moderate size in most rows, possibly larger in a few. `text_mask`: vision and text tokens come in runs of 16 aligned tokens.
All inputs are finite; a program needn't handle non-finite values.
Results may differ from a plain program's by a relative error of at most 0.0003.
Values may be sent and summed in bfloat16 or wider, within the bound.
No kernel may reach another device: no remote copies, remote signals or barrier semaphores. Data moves between devices by JAX's collectives and lax.ppermute only.
A program may use at most 128 MiB of HBM per device.

v0:
```python
import jax
import jax.numpy as jnp
from jax import lax
from jax.sharding import PartitionSpec as P


def combined_all(part, axis, combine):
    gathered = jax.tree.map(lambda a: lax.all_gather(a, axis), part)

    def take(source):
        return jax.tree.map(lambda a: lax.dynamic_index_in_dim(a, source, 0, False), gathered)

    return lax.fori_loop(
        1, lax.axis_size(axis), lambda source, state: combine(state, take(source)), take(0)
    )


def shards(hidden, out_weight, labels, text_mask):
    gathered = lax.all_gather(hidden, "vocab", axis=0, tiled=True)
    width_here = out_weight.shape[1]
    first_column = lax.axis_index("vocab") * width_here
    weight_full = lax.all_gather(out_weight, "dp", axis=0, tiled=True)
    logits = jnp.dot(gathered, weight_full, preferred_element_type=jnp.float32)
    columns = jnp.arange(width_here, dtype=jnp.int32)
    local_targets = labels - first_column
    picked = jnp.sum(
        jnp.where(columns[None, :] == local_targets[:, None], logits, jnp.float32(0.0)), axis=1
    )
    local_top = jnp.max(logits, axis=1)
    weights_text = text_mask.astype(jnp.float32)
    tally = lax.psum(jnp.sum(weights_text), "dp")
    local_total = jnp.sum(jnp.exp(logits - local_top[:, None]), axis=1)

    def combine(first, second):
        upper = jnp.maximum(first[0], second[0])
        summed = first[1] * jnp.exp(first[0] - upper) + second[1] * jnp.exp(second[0] - upper)
        return (upper, summed, first[2] + second[2])

    row_top, exp_total, label_logit = combined_all(
        (local_top, local_total, picked), "vocab", combine
    )
    token_loss = weights_text * (row_top + jnp.log(exp_total) - label_logit)
    loss_sum = lax.psum(jnp.sum(token_loss), "dp")
    mean_loss = loss_sum / jnp.maximum(tally, jnp.float32(1.0))
    return (token_loss, mean_loss)


def solution(mesh):
    in_specs = (P(("dp", "vocab"), None), P("dp", "vocab"), P("dp"), P("dp"))
    out_specs = (P("dp"), P())
    return jax.shard_map(shards, mesh=mesh, in_specs=in_specs, out_specs=out_specs, check_vma=False)
```

profile of v0, /device:TPU:0, one launch (start us, length us, event | category | flops | bytes accessed | tf_op | source)
XLA Modules:
  0.0 480.1 jit_solution(2350190988107568957)
XLA Ops:
  7.2 0.0 all-gather.9.cloned.1.call-start
  7.2 0.7 all-gather.9.cloned.1.call-update
  7.9 0.0 all-gather.11.cloned.1.call-start
  7.9 0.7 all-gather.11.cloned.1.call-update
  8.7 0.7 broadcast_subtract_fusion
  9.3 44.3 %all-gather.9.cloned.1.call-done = bf16[640,4096]{1,0:T(8,128)(2,1)} async-done(((bf16[80,4096]{1,0:T(8,128)(2,1)}), bf16[640,4096]{1,0:T(8,128)(2,1)}) %all-gather.9.cloned.1.call-update) | async-done | bytes 5242896 | tf_op jit(solution)/shard_map/all_gather | solution.py:19
  53.6 358.4 %all-gather.11.cloned.1.call-done = bf16[4096,2560]{1,0:T(8,128)(2,1)} async-done(((bf16[1024,2560]{1,0:T(8,128)(2,1)}), bf16[4096,2560]{1,0:T(8,128)(2,1)}) %all-gather.11.cloned.1.call-update) | async-done | bytes 20971536 | tf_op jit(solution)/shard_map/all_gather | solution.py:22
  412.0 18.6 %fusion.1 = (f32[640]{0:T(1024)S(1)}, f32[640,2560]{1,0:T(8,128)S(1)}) fusion(bf16[640,4096]{1,0:T(8,128)(2,1)} %all-gather.9.cloned.1.call-done, bf16[4096,2560]{1,0:T(8,128)(2,1)} %all-gather.11.cloned.1.call-done), kind=kOutput, calls=%fused_computation.17 | convolution fusion | flops 13423410176 | bytes 32770560 | tf_op jit(solution)/shard_map/dot_general | solution.py:23
  430.6 0.0 copy-start
  430.6 2.2 select_reduce_fusion
  432.8 9.0 %all-gather.5 = f32[8,1,640]{2,1,0:T(1,128)S(1)} all-gather(f32[1,1,640]{2,1,0:T(1,128)S(1)} %reshape.19), channel_id=4, replica_groups=mesh['dp'=4,'vocab'=8] {'vocab'}, dimensions={0}, use_global_device_ids=true | all-gather | bytes 23040 | tf_op jit(solution)/shard_map/all_gather | solution.py:8
  441.9 9.0 %all-gather.4 = f32[8,1,640]{2,1,0:T(1,128)S(1)} all-gather(f32[1,1,640]{2,1,0:T(1,128)S(1)} %reshape.17), channel_id=3, replica_groups=mesh['dp'=4,'vocab'=8] {'vocab'}, dimensions={0}, use_global_device_ids=true | all-gather | bytes 23040 | tf_op jit(solution)/shard_map/all_gather | solution.py:8
  450.9 8.1 %all-gather.3 = f32[8,1,640]{2,1,0:T(1,128)S(1)} all-gather(f32[1,1,640]{2,1,0:T(1,128)S(1)} %reshape.15), channel_id=2, replica_groups=mesh['dp'=4,'vocab'=8] {'vocab'}, dimensions={0}, use_global_device_ids=true | all-gather | bytes 23040 | tf_op jit(solution)/shard_map/all_gather | solution.py:8
  459.0 0.8 while.19
  459.8 0.0 copy-done
  459.8 1.3 fusion
  461.1 9.8 %all-reduce = (f32[]{:T(128)}, f32[]{:T(128)}) all-reduce(f32[]{:T(128)} %get-tuple-element.203, f32[]{:T(128)} %get-tuple-element.207), channel_id=1, replica_groups=mesh['dp'=4,'vocab'=8] {'dp'}, use_global_device_ids=true, to_apply=%region_6.7 | all-reduce | flops 2 | bytes 16 | tf_op jit(solution)/shard_map/psum | solution.py:43
  (37 shorter events, 0.5 us)
Async XLA Ops:
  7.2 46.4 %all-gather.9.cloned.1.call-start = ((), (), s32[]{:S(2)}) async-start(), calls=%async_computation | async-start | bytes 5898240 | tf_op jit(solution)/shard_map/all_gather | solution.py:19
  7.9 404.1 %all-gather.11.cloned.1.call-start = ((), (), s32[]{:S(2)}) async-start(), calls=%async_computation.1 | async-start | bytes 26214400 | tf_op jit(solution)/shard_map/all_gather | solution.py:22
  430.6 29.2 %copy-start = (s32[640]{0:T(1024)S(1)}, s32[640]{0:T(1024)}, u32[]{:S(2)}) copy-start(s32[640]{0:T(1024)} %param.9) | copy-start | bytes 7684
Sparse Core Ops, SparseCore 0:
  9.9 43.6 all-gather.8
  55.2 356.8 all-gather.10
where the time goes:
time: 480 us
  waiting for transfers between devices  404 us (84%)
  blocking collectives  36 us (8%)
  matrix products  18.6 us (4%)
  between operations  16.5 us (3%)
    all_gather x1, waiting for transfers between devices, shards(): weight_full = lax.all_gather(out_weight, 'dp', axis=0, tiled=True)  358 us
    all_gather x1, waiting for transfers between devices, shards(): gathered = lax.all_gather(hidden, 'vocab', axis=0, tiled=True)  44.3 us
    all_gather x3, blocking collectives, combined_all(): gathered = jax.tree.map(lambda a: lax.all_gather(a, axis), part)  26.2 us
    dot_general x1, matrix products, shards(): logits = jnp.dot(gathered, weight_full, preferred_element_type=jnp.float32)  18.6 us
    psum x1, blocking collectives, shards(): loss_sum = lax.psum(jnp.sum(token_loss), 'dp')  9.84 us
  transfers between devices with their start and end apart: 2, of which 2 were waited for; matrix products, arithmetic and copies ran while one was open for 0% of the time, Pallas kernels for 0%

commit v1 on v0

--- a/solution.py
+++ b/solution.py
@@ -16,7 +16,14 @@
 
 
 def shards(hidden, out_weight, labels, text_mask):
-    gathered = lax.all_gather(hidden, "vocab", axis=0, tiled=True)
+    devices = lax.axis_size("vocab")
+    route = [(i, (i + 1) % devices) for i in range(devices)]
+    parts = [hidden]
+    for far in range(1, devices):
+        parts = [lax.ppermute(parts[0], "vocab", route), *parts]
+    full = jnp.concatenate(parts, axis=0)
+    places = (lax.axis_index("vocab") + 1) * parts[-1].shape[0]
+    gathered = jnp.roll(full, places, axis=0)
     width_here = out_weight.shape[1]
     first_column = lax.axis_index("vocab") * width_here
     weight_full = lax.all_gather(out_weight, "dp", axis=0, tiled=True)

time: 480 us -> 438 us (0.912)
  waiting for transfers between devices: 404 us -> 340 us
  local copies, waits for them, and re-layouts: 0.4 us -> 21.1 us
    all_gather x1, waiting for transfers between devices: 358 us -> 263 us  [shards(): weight_full = lax.all_gather(out_weight, 'dp', axis=0, tiled=True)]
    ppermute x0 -> x7, waiting for transfers between devices: none -> 76.5 us  [shards(): parts = [lax.ppermute(parts[0], 'vocab', route), *parts]]
    all_gather x1 -> x0, waiting for transfers between devices: 44.3 us -> none  [shards(): gathered = lax.all_gather(hidden, 'vocab', axis=0, tiled=True)]
    unnamed x8 -> x29, local copies, waits for them, and re-layouts: 0.03 us -> 19.8 us
  transfers between devices with their start and end apart: 2 -> 8, of which waited for: 2 -> 8; matrix products, arithmetic and copies ran while one was open for 0% -> 5% of each run, Pallas kernels for 0% -> 0%
where the time goes in v1:
time: 438 us; the launch traced here: 437 us
  waiting for transfers between devices  340 us (78%)
  blocking collectives  36 us (8%)
  local copies, waits for them, and re-layouts  21.1 us (5%)
  matrix products  18.6 us (4%)
  between operations  16.5 us (4%)
    all_gather x1, waiting for transfers between devices, shards(): weight_full = lax.all_gather(out_weight, 'dp', axis=0, tiled=True)  263 us
    ppermute x7, waiting for transfers between devices, shards(): parts = [lax.ppermute(parts[0], 'vocab', route), *parts]  76.5 us
    all_gather x3, blocking collectives, combined_all(): gathered = jax.tree.map(lambda a: lax.all_gather(a, axis), part)  26.2 us
    unnamed x29, local copies, waits for them, and re-layouts  19.8 us
    dot_general x1, matrix products, shards(): logits = jnp.dot(gathered, weight_full, preferred_element_type=jnp.float32)  18.6 us
    psum x1, blocking collectives, shards(): loss_sum = lax.psum(jnp.sum(token_loss), 'dp')  9.85 us
  transfers between devices with their start and end apart: 8, of which 8 were waited for; matrix products, arithmetic and copies ran while one was open for 5% of the time, Pallas kernels for 0%

profile of v1, /device:TPU:0, one launch (start us, length us, event | category | flops | bytes accessed | tf_op | source)
XLA Modules:
  0.0 437.3 jit_solution(4332656094396267264)
XLA Ops:
  8.5 11.3 %collective-permute-done = bf16[80,4096]{1,0:T(8,128)(2,1)S(1)} collective-permute-done((bf16[80,4096]{1,0:T(8,128)(2,1)}, bf16[80,4096]{1,0:T(8,128)(2,1)S(1)}, u32[]{:S(2)}, u32[]{:S(2)}) %collective-permute-start) | collective-permute-done | bytes 655392 | tf_op jit(solution)/shard_map/ppermute | solution.py:23
  19.8 10.9 %collective-permute-done.1 = bf16[80,4096]{1,0:T(8,128)(2,1)S(1)} collective-permute-done((bf16[80,4096]{1,0:T(8,128)(2,1)S(1)}, bf16[80,4096]{1,0:T(8,128)(2,1)S(1)}, u32[]{:S(2)}, u32[]{:S(2)}) %collective-permute-start.1) | collective-permute-done | bytes 655392 | tf_op jit(solution)/shard_map/ppermute | solution.py:23
  30.7 10.9 %collective-permute-done.2 = bf16[80,4096]{1,0:T(8,128)(2,1)S(1)} collective-permute-done((bf16[80,4096]{1,0:T(8,128)(2,1)S(1)}, bf16[80,4096]{1,0:T(8,128)(2,1)S(1)}, u32[]{:S(2)}, u32[]{:S(2)}) %collective-permute-start.2) | collective-permute-done | bytes 655392 | tf_op jit(solution)/shard_map/ppermute | solution.py:23
  41.6 10.9 %collective-permute-done.3 = bf16[80,4096]{1,0:T(8,128)(2,1)S(1)} collective-permute-done((bf16[80,4096]{1,0:T(8,128)(2,1)S(1)}, bf16[80,4096]{1,0:T(8,128)(2,1)S(1)}, u32[]{:S(2)}, u32[]{:S(2)}) %collective-permute-start.3) | collective-permute-done | bytes 655392 | tf_op jit(solution)/shard_map/ppermute | solution.py:23
  52.5 10.9 %collective-permute-done.4 = bf16[80,4096]{1,0:T(8,128)(2,1)S(1)} collective-permute-done((bf16[80,4096]{1,0:T(8,128)(2,1)S(1)}, bf16[80,4096]{1,0:T(8,128)(2,1)S(1)}, u32[]{:S(2)}, u32[]{:S(2)}) %collective-permute-start.4) | collective-permute-done | bytes 655392 | tf_op jit(solution)/shard_map/ppermute | solution.py:23
  63.4 0.8 copy-done.1
  64.3 11.0 %collective-permute-done.5 = bf16[80,4096]{1,0:T(8,128)(2,1)} collective-permute-done((bf16[80,4096]{1,0:T(8,128)(2,1)S(1)}, bf16[80,4096]{1,0:T(8,128)(2,1)}, u32[]{:S(2)}, u32[]{:S(2)}) %collective-permute-start.5) | collective-permute-done | bytes 655392 | tf_op jit(solution)/shard_map/ppermute | solution.py:23
  76.1 10.5 %collective-permute-done.6 = bf16[80,4096]{1,0:T(8,128)(2,1)} collective-permute-done((bf16[80,4096]{1,0:T(8,128)(2,1)}, bf16[80,4096]{1,0:T(8,128)(2,1)}, u32[]{:S(2)}, u32[]{:S(2)}) %collective-permute-start.6) | collective-permute-done | bytes 655392 | tf_op jit(solution)/shard_map/ppermute | solution.py:23
  86.5 2.0 constant_dynamic-update-slice_fusion.15
  88.5 2.0 constant_dynamic-update-slice_fusion.14
  90.5 2.0 constant_dynamic-update-slice_fusion.13
  92.5 0.9 constant_dynamic-update-slice_fusion.12
  93.4 0.9 constant_dynamic-update-slice_fusion.11
  94.3 0.9 constant_dynamic-update-slice_fusion.10
  95.2 0.9 constant_dynamic-update-slice_fusion.9
  96.1 1.0 constant_dynamic-update-slice_fusion.8
  97.1 2.0 constant_dynamic-update-slice_fusion.7
  99.0 2.0 constant_dynamic-update-slice_fusion.6
  101.0 0.9 constant_dynamic-update-slice_fusion.5
  101.9 0.9 constant_dynamic-update-slice_fusion.4
  102.8 0.9 constant_dynamic-update-slice_fusion.3
  103.7 0.9 constant_dynamic-update-slice_fusion.2
  104.6 0.9 constant_dynamic-update-slice_fusion.1
  105.5 0.9 constant_dynamic-update-slice_fusion
  106.4 262.8 %all-gather.8.cloned.1.call-done = bf16[4096,2560]{1,0:T(8,128)(2,1)} async-done(((bf16[1024,2560]{1,0:T(8,128)(2,1)}), bf16[4096,2560]{1,0:T(8,128)(2,1)}) %all-gather.8.cloned.1.call-update) | async-done | bytes 20971536 | tf_op jit(solution)/shard_map/all_gather | solution.py:29
  369.1 18.6 %fusion.4 = (f32[640]{0:T(1024)S(1)}, f32[640,2560]{1,0:T(8,128)S(1)}) fusion(bf16[4096,2560]{1,0:T(8,128)(2,1)} %all-gather.8.cloned.1.call-done, bf16[1280,4096]{1,0:T(8,128)(2,1)} %constant_dynamic-update-slice_fusion, s32[]{:T(128)S(6)} %select_n.34), kind=kOutput, calls=%fused_computation.36 | convolution fusion | flops 13423410176 | bytes 32770564 | tf_op jit(solution)/shard_map/dot_general | solution.py:30
  387.8 2.2 select_reduce_fusion
  389.9 9.0 %all-gather.5 = f32[8,1,640]{2,1,0:T(1,128)S(1)} all-gather(f32[1,1,640]{2,1,0:T(1,128)S(1)} %reshape.19), channel_id=4, replica_groups=mesh['dp'=4,'vocab'=8] {'vocab'}, dimensions={0}, use_global_device_ids=true | all-gather | bytes 23040 | tf_op jit(solution)/shard_map/all_gather | solution.py:8
  399.0 9.0 %all-gather.4 = f32[8,1,640]{2,1,0:T(1,128)S(1)} all-gather(f32[1,1,640]{2,1,0:T(1,128)S(1)} %reshape.17), channel_id=3, replica_groups=mesh['dp'=4,'vocab'=8] {'vocab'}, dimensions={0}, use_global_device_ids=true | all-gather | bytes 23040 | tf_op jit(solution)/shard_map/all_gather | solution.py:8
  408.0 8.2 %all-gather.3 = f32[8,1,640]{2,1,0:T(1,128)S(1)} all-gather(f32[1,1,640]{2,1,0:T(1,128)S(1)} %reshape.15), channel_id=2, replica_groups=mesh['dp'=4,'vocab'=8] {'vocab'}, dimensions={0}, use_global_device_ids=true | all-gather | bytes 23040 | tf_op jit(solution)/shard_map/all_gather | solution.py:8
  417.0 1.3 fusion.3
  418.3 9.9 %all-reduce = (f32[]{:T(128)}, f32[]{:T(128)}) all-reduce(f32[]{:T(128)} %get-tuple-element.203, f32[]{:T(128)} %get-tuple-element.207), channel_id=1, replica_groups=mesh['dp'=4,'vocab'=8] {'dp'}, use_global_device_ids=true, to_apply=%region_6.7 | all-reduce | flops 2 | bytes 16 | tf_op jit(solution)/shard_map/psum | solution.py:50
  (55 shorter events, 3.3 us)
Async XLA Ops:
  7.2 89.0 %copy-start = (bf16[80,4096]{1,0:T(8,128)(2,1)S(1)}, bf16[80,4096]{1,0:T(8,128)(2,1)}, u32[]{:S(2)}) copy-start(bf16[80,4096]{1,0:T(8,128)(2,1)} %param.6) | copy-start | bytes 1966084
  7.2 362.0 %all-gather.8.cloned.1.call-start = ((), (), s32[]{:S(2)}) async-start(), calls=%async_computation | async-start | bytes 26214400 | tf_op jit(solution)/shard_map/all_gather | solution.py:29
  7.9 11.9 %collective-permute-start = (bf16[80,4096]{1,0:T(8,128)(2,1)}, bf16[80,4096]{1,0:T(8,128)(2,1)S(1)}, u32[]{:S(2)}, u32[]{:S(2)}) collective-permute-start(bf16[80,4096]{1,0:T(8,128)(2,1)} %param.6), channel_id=1, source_target_pairs={{0,1},{1,2},{2,3},{3,4},{4,5},{5,6},{6,7},{7,0},{8,9},{9,10},{10,1... | collective-permute-start | bytes 1966088 | tf_op jit(solution)/shard_map/ppermute | solution.py:23
  19.8 10.9 %collective-permute-start.1 = (bf16[80,4096]{1,0:T(8,128)(2,1)S(1)}, bf16[80,4096]{1,0:T(8,128)(2,1)S(1)}, u32[]{:S(2)}, u32[]{:S(2)}) collective-permute-start(bf16[80,4096]{1,0:T(8,128)(2,1)S(1)} %collective-permute-done), channel_id=1, source_target_pairs={{0,1},{1,2},{2,3},{3,4},{4,5},{5,6},{6,7},{7,0},{8,9},{9,10},{10,1... | collective-permute-start | bytes 1966088 | tf_op jit(solution)/shard_map/ppermute | solution.py:23
  30.7 10.9 %collective-permute-start.2 = (bf16[80,4096]{1,0:T(8,128)(2,1)S(1)}, bf16[80,4096]{1,0:T(8,128)(2,1)S(1)}, u32[]{:S(2)}, u32[]{:S(2)}) collective-permute-start(bf16[80,4096]{1,0:T(8,128)(2,1)S(1)} %collective-permute-done.1), channel_id=1, source_target_pairs={{0,1},{1,2},{2,3},{3,4},{4,5},{5,6},{6,7},{7,0},{8,9},{9,10},{10,1... | collective-permute-start | bytes 1966088 | tf_op jit(solution)/shard_map/ppermute | solution.py:23
  41.6 10.9 %collective-permute-start.3 = (bf16[80,4096]{1,0:T(8,128)(2,1)S(1)}, bf16[80,4096]{1,0:T(8,128)(2,1)S(1)}, u32[]{:S(2)}, u32[]{:S(2)}) collective-permute-start(bf16[80,4096]{1,0:T(8,128)(2,1)S(1)} %collective-permute-done.2), channel_id=1, source_target_pairs={{0,1},{1,2},{2,3},{3,4},{4,5},{5,6},{6,7},{7,0},{8,9},{9,10},{10,1... | collective-permute-start | bytes 1966088 | tf_op jit(solution)/shard_map/ppermute | solution.py:23
  52.5 10.9 %collective-permute-start.4 = (bf16[80,4096]{1,0:T(8,128)(2,1)S(1)}, bf16[80,4096]{1,0:T(8,128)(2,1)S(1)}, u32[]{:S(2)}, u32[]{:S(2)}) collective-permute-start(bf16[80,4096]{1,0:T(8,128)(2,1)S(1)} %collective-permute-done.3), channel_id=1, source_target_pairs={{0,1},{1,2},{2,3},{3,4},{4,5},{5,6},{6,7},{7,0},{8,9},{9,10},{10,1... | collective-permute-start | bytes 1966088 | tf_op jit(solution)/shard_map/ppermute | solution.py:23
  63.4 0.9 copy-start.1
  64.3 11.0 %collective-permute-start.5 = (bf16[80,4096]{1,0:T(8,128)(2,1)S(1)}, bf16[80,4096]{1,0:T(8,128)(2,1)}, u32[]{:S(2)}, u32[]{:S(2)}) collective-permute-start(bf16[80,4096]{1,0:T(8,128)(2,1)S(1)} %collective-permute-done.4), channel_id=1, source_target_pairs={{0,1},{1,2},{2,3},{3,4},{4,5},{5,6},{6,7},{7,0},{8,9},{9,10},{10,1... | collective-permute-start | bytes 1966088 | tf_op jit(solution)/shard_map/ppermute | solution.py:23
  75.3 11.2 %collective-permute-start.6 = (bf16[80,4096]{1,0:T(8,128)(2,1)}, bf16[80,4096]{1,0:T(8,128)(2,1)}, u32[]{:S(2)}, u32[]{:S(2)}) collective-permute-start(bf16[80,4096]{1,0:T(8,128)(2,1)} %collective-permute-done.5), channel_id=1, source_target_pairs={{0,1},{1,2},{2,3},{3,4},{4,5},{5,6},{6,7},{7,0},{8,9},{9,10},{10,1... | collective-permute-start | bytes 1966088 | tf_op jit(solution)/shard_map/ppermute | solution.py:23
  75.3 25.7 %copy-start.2 = (bf16[80,4096]{1,0:T(8,128)(2,1)S(1)}, bf16[80,4096]{1,0:T(8,128)(2,1)}, u32[]{:S(2)}) copy-start(bf16[80,4096]{1,0:T(8,128)(2,1)} %copy-done.1) | copy-start | bytes 1966084
  106.4 310.6 %copy-start.3 = (s32[640]{0:T(1024)S(1)}, s32[640]{0:T(1024)}, u32[]{:S(2)}) copy-start(s32[640]{0:T(1024)} %param.9) | copy-start | bytes 7684
Sparse Core Ops, SparseCore 0:
  9.6 359.5 all-gather.7
